TPU v7x, 32 devices: a whole 2x2x4 slice. The times are simulated.
32 devices in a mesh: seq: 8 (over z, core), feat: 4 (over y, x).
Axes of the slice: x: 2, y: 2, z: 4, core: 2. Of those that a mesh axis runs over, the one named last changes fastest.
Arguments:
- activations: bfloat16 [2048, 6144], P('seq', 'feat'), may hold values from -15 to 15
- ridge_scale: float32 [], replicated, may hold values from 0.5 to 2
Outputs:
- whitened: bfloat16 [2048, 6144], P('seq', 'feat')
All inputs are finite; a program needn't handle non-finite values.
Results may differ from a plain program's by a relative error of at most 0.0033.
Values sent between devices are 32-bit elements; how exact they have to be, the bound alone decides.
A program may use at most 128 MiB of HBM per device.

v0:
```python
import jax
import jax.numpy as jnp
from jax import lax
from jax.sharding import PartitionSpec as P

RANK = 128
ROOT_STEPS = 12


precise = lax.Precision.HIGHEST


def partner_2(block, axis, bit):
    count = lax.axis_size(axis)
    route = []
    for low in range(count):
        high = low | 1 << bit
        if high != low and high < count:
            route += [(low, high), (high, low)]
    return lax.ppermute(block, axis, route)


def product(left_matrix, right_matrix):
    return jnp.dot(left_matrix, right_matrix, precision=precise)


def reduce_gram(stacked_gram):
    rank_size = stacked_gram.shape[0] // 2
    identity = jnp.eye(rank_size, dtype=stacked_gram.dtype)
    subspace = jnp.concatenate([identity, identity], axis=0) * 0.7071067811865476
    image_cols = product(stacked_gram, subspace)
    factor = jnp.linalg.cholesky(product(image_cols.T, image_cols))
    subspace = jax.scipy.linalg.solve_triangular(factor, image_cols.T, lower=True).T
    quotient = product(subspace.T, product(stacked_gram, subspace))
    quotient = 0.5 * (quotient + quotient.T)
    tail_mass = (jnp.trace(stacked_gram) - jnp.trace(quotient)) / rank_size
    root_factor = jnp.linalg.cholesky(quotient)
    inner_gram = product(root_factor.T, root_factor) + tail_mass * identity
    lower_factor = jnp.linalg.cholesky(inner_gram)
    return jax.scipy.linalg.solve_triangular(
        lower_factor, product(root_factor.T, subspace.T), lower=True
    )


def combine(earlier, later):
    own_gram, cross_gram, last_gram = lax.psum(
        (product(earlier, earlier.T), product(earlier, later.T), product(later, later.T)), "feat"
    )
    stacked_gram = jnp.concatenate(
        [jnp.concatenate([own_gram, cross_gram], 1), jnp.concatenate([cross_gram.T, last_gram], 1)],
        0,
    )
    mixing = reduce_gram(stacked_gram)
    return product(mixing, jnp.concatenate([earlier, later], 0))


def square_root(matrix):
    identity = jnp.eye(matrix.shape[0], dtype=matrix.dtype)
    norm_size = jnp.sqrt(jnp.sum(matrix * matrix))
    current = matrix / norm_size
    partner = identity
    for repeat in range(ROOT_STEPS):
        middle = 1.5 * identity - 0.5 * product(partner, current)
        current = product(current, middle)
        partner = product(middle, partner)
    return current * jnp.sqrt(norm_size)


def on_device(activations, ridge_scale):
    width = activations.shape[1]
    block_count = activations.shape[0] // (2 * RANK)
    block_rows = activations.reshape(block_count, 2 * RANK, width)
    partial_grams = jnp.einsum(
        "bik,bjk->bij", block_rows, block_rows, preferred_element_type=jnp.float32
    )
    slab_grams = lax.psum(partial_grams, "feat")
    mixtures = jax.vmap(reduce_gram)(slab_grams)
    sketches = jnp.einsum(
        "bij,bjk->bik", mixtures, block_rows.astype(jnp.float32), precision=precise
    )
    slab_sketch = sketches[0]
    levels = lax.axis_size("seq").bit_length() - 1
    seq_index = lax.axis_index("seq")
    tree_block = slab_sketch
    prefix = slab_sketch
    for tree_level in range(levels):
        partner = partner_2(tree_block, "seq", tree_level)
        merged = combine(partner, prefix)
        has_bit = seq_index // (1 << tree_level) % 2 == 1
        prefix = jnp.where(has_bit, merged, prefix)
        if tree_level + 1 < levels:
            tree_block = combine(tree_block, partner)
    seen_rows = ((seq_index + 1) * activations.shape[0]).astype(jnp.float32)
    scaled = prefix * lax.rsqrt(seen_rows * ridge_scale)
    half_basis = scaled.astype(jnp.bfloat16)
    small_gram, projection = lax.psum(
        (
            product(scaled, scaled.T),
            jnp.dot(activations, half_basis.T, preferred_element_type=jnp.float32),
        ),
        "feat",
    )
    identity = jnp.eye(small_gram.shape[0], dtype=small_gram.dtype)
    shifted = identity + small_gram
    total_gram = shifted + square_root(shifted)
    total_gram = 0.5 * (total_gram + total_gram.T)
    coefficients = jax.scipy.linalg.cho_solve(
        (jnp.linalg.cholesky(total_gram), True), projection.T
    ).T
    restored = jnp.dot(
        coefficients.astype(jnp.bfloat16), half_basis, preferred_element_type=jnp.float32
    )
    return ((activations.astype(jnp.float32) - restored) * lax.rsqrt(ridge_scale)).astype(
        jnp.bfloat16
    )


def solution(mesh):
    placed = (P("seq", "feat"), P())
    return jax.shard_map(
        on_device, mesh=mesh, in_specs=placed, out_specs=P("seq", "feat"), check_vma=False
    )
```

profile of v0, /device:TPU:0, one launch (start us, length us, event | category | flops | bytes accessed | tf_op | source)
XLA Modules:
  0.0 740.0 jit_solution(10634055439625661038)
XLA Ops:
  9.2 46.9 %all-reduce.10.cloned.1.call-done = f32[1,256,256]{2,1,0:T(8,128)} async-done(((f32[1,256,256]{2,1,0:T(8,128)}), f32[1,256,256]{2,1,0:T(8,128)}) %all-reduce.10.cloned.1.call-update) | async-done | bytes 262160 | tf_op jit(solution)/shard_map/psum | solution.py:76
  58.0 11.7 %custom-call.29 = f32[1,128,128]{2,1,0:T(8,128)S(1)} custom-call(f32[1,128,128]{2,1,0:T(8,128)S(1)} %fusion.75), custom_call_target="Cholesky" | custom-call | tf_op jit(solution)/shard_map/vmap(jit(cholesky))/cholesky | solution.py:32
  71.0 9.8 %custom-call.30 = f32[1,1,128,128]{2,3,1,0:T(8,128)S(1)} custom-call(f32[1,1,128,128]{3,2,1,0:T(8,128)S(1)} %fusion.60), custom_call_target="InvertDiagBlocksLowerTriangular" | custom-call | tf_op jit(solution)/shard_map/vmap(jit(_solve_triangular))/triangular_solve | solution.py:33
  82.7 11.7 %custom-call.31 = f32[1,128,128]{2,1,0:T(8,128)S(1)} custom-call(f32[1,128,128]{2,1,0:T(8,128)S(1)} %fusion.121), custom_call_target="Cholesky" | custom-call | tf_op jit(solution)/shard_map/vmap(jit(cholesky))/cholesky | solution.py:37
  99.3 11.7 %custom-call.32 = f32[1,128,128]{2,1,0:T(8,128)S(1)} custom-call(f32[1,128,128]{2,1,0:T(8,128)S(1)} %fusion.73), custom_call_target="Cholesky" | custom-call | tf_op jit(solution)/shard_map/vmap(jit(cholesky))/cholesky | solution.py:39
  129.9 43.2 %all-reduce.18.cloned.1.call-done = (f32[128,128]{1,0:T(8,128)}, f32[128,128]{1,0:T(8,128)}, f32[128,128]{1,0:T(8,128)}, f32[128,128]{0,1:T(8,128)}) async-done(((f32[128,128]{1,0:T(8,128)}, f32[128,128]{1,0:T(8,128)}, f32[128,128]{1,0:T(8,128)}, f32[128,128]{0,1:T(8,128)}), (f32[128,128]{1,0:T(8,128)}, f32[128,128]{1,0:T(8,128)}, f32[128,128]{1,0:T(8,128)}, ...) | async-done | bytes 262160 | tf_op jit(solution)/shard_map/psum | solution.py:46
  178.1 11.7 %cholesky.404 = f32[128,128]{1,0:T(8,128)S(1)} custom-call(f32[128,128]{1,0:T(8,128)S(1)} %fusion.101), custom_call_target="Cholesky" | custom-call | tf_op jit(solution)/shard_map/jit(cholesky)/cholesky | solution.py:32
  202.7 12.1 %cholesky.415 = f32[128,128]{1,0:T(8,128)S(1)} custom-call(f32[128,128]{1,0:T(8,128)S(1)} %fusion.98), custom_call_target="Cholesky" | custom-call | tf_op jit(solution)/shard_map/jit(cholesky)/cholesky | solution.py:37
  218.7 11.7 %cholesky.426 = f32[128,128]{1,0:T(8,128)S(1)} custom-call(f32[128,128]{1,0:T(8,128)S(1)} %fusion.97), custom_call_target="Cholesky" | custom-call | tf_op jit(solution)/shard_map/jit(cholesky)/cholesky | solution.py:39
  242.1 11.7 %cholesky.338 = f32[128,128]{1,0:T(8,128)S(1)} custom-call(f32[128,128]{1,0:T(8,128)S(1)} %fusion.115), custom_call_target="Cholesky" | custom-call | tf_op jit(solution)/shard_map/jit(cholesky)/cholesky | solution.py:32
  255.2 10.0 %custom-call.34 = f32[1,128,128]{1,2,0:T(8,128)S(1)} custom-call(f32[1,128,128]{2,1,0:T(8,128)S(1)} %fusion.62), custom_call_target="InvertDiagBlocksLowerTriangular" | custom-call | tf_op jit(solution)/shard_map/jit(_solve_triangular)/triangular_solve/custom-call.3 | solution.py:33
  267.0 11.7 %cholesky.349 = f32[128,128]{1,0:T(8,128)S(1)} custom-call(f32[128,128]{1,0:T(8,128)S(1)} %fusion.112), custom_call_target="Cholesky" | custom-call | tf_op jit(solution)/shard_map/jit(cholesky)/cholesky | solution.py:37
  282.5 11.7 %cholesky.360 = f32[128,128]{1,0:T(8,128)S(1)} custom-call(f32[128,128]{1,0:T(8,128)S(1)} %fusion.111), custom_call_target="Cholesky" | custom-call | tf_op jit(solution)/shard_map/jit(cholesky)/cholesky | solution.py:39
  295.6 10.2 %custom-call.35 = f32[1,128,128]{1,2,0:T(8,128)S(1)} custom-call(f32[1,128,128]{2,1,0:T(8,128)S(1)} %fusion.63), custom_call_target="InvertDiagBlocksLowerTriangular" | custom-call | tf_op jit(solution)/shard_map/jit(_solve_triangular)/triangular_solve/custom-call.3 | solution.py:40
  312.8 13.1 %collective-permute-done.1 = f32[128,1536]{1,0:T(8,128)S(1)} collective-permute-done((f32[128,1536]{1,0:T(8,128)S(1)}, f32[128,1536]{1,0:T(8,128)S(1)}, u32[]{:S(2)}, u32[]{:S(2)}) %collective-permute-start.1) | collective-permute-done | bytes 786464 | tf_op jit(solution)/shard_map/ppermute | solution.py:20
  330.4 44.5 %all-reduce.16.cloned.1.call-done = (f32[128,128]{1,0:T(8,128)}, f32[128,128]{0,1:T(8,128)}, f32[128,128]{0,1:T(8,128)}, f32[128,128]{0,1:T(8,128)}, f32[128,128]{0,1:T(8,128)}) async-done(((f32[128,128]{1,0:T(8,128)}, f32[128,128]{0,1:T(8,128)}, f32[128,128]{0,1:T(8,128)}, f32[128,128]{0,1:T(8,128)}, f32[128,128]{0,1:T(8,128)}), (f32[128,128]{1,0:T(8,128)}, f32[128,128]{0,1:T(8,128)}, ...) | async-done | bytes 327696 | tf_op jit(solution)/shard_map/psum | solution.py:46
  378.5 11.7 %cholesky.437 = f32[128,128]{1,0:T(8,128)S(1)} custom-call(f32[128,128]{1,0:T(8,128)S(1)} %fusion.94), custom_call_target="Cholesky" | custom-call | tf_op jit(solution)/shard_map/jit(cholesky)/cholesky | solution.py:32
  403.2 11.7 %cholesky.448 = f32[128,128]{1,0:T(8,128)S(1)} custom-call(f32[128,128]{1,0:T(8,128)S(1)} %fusion.91), custom_call_target="Cholesky" | custom-call | tf_op jit(solution)/shard_map/jit(cholesky)/cholesky | solution.py:37
  418.9 11.7 %cholesky.459 = f32[128,128]{1,0:T(8,128)S(1)} custom-call(f32[128,128]{1,0:T(8,128)S(1)} %fusion.90), custom_call_target="Cholesky" | custom-call | tf_op jit(solution)/shard_map/jit(cholesky)/cholesky | solution.py:39
  432.5 11.7 %cholesky.371 = f32[128,128]{1,0:T(8,128)S(1)} custom-call(f32[128,128]{1,0:T(8,128)S(1)} %fusion.108), custom_call_target="Cholesky" | custom-call | tf_op jit(solution)/shard_map/jit(cholesky)/cholesky | solution.py:32
  445.7 9.8 %custom-call.36 = f32[1,128,128]{1,2,0:T(8,128)S(1)} custom-call(f32[1,128,128]{2,1,0:T(8,128)S(1)} %fusion.64), custom_call_target="InvertDiagBlocksLowerTriangular" | custom-call | tf_op jit(solution)/shard_map/jit(_solve_triangular)/triangular_solve/custom-call.3 | solution.py:33
  458.0 11.7 %cholesky.382 = f32[128,128]{1,0:T(8,128)S(1)} custom-call(f32[128,128]{1,0:T(8,128)S(1)} %fusion.105), custom_call_target="Cholesky" | custom-call | tf_op jit(solution)/shard_map/jit(cholesky)/cholesky | solution.py:37
  474.5 11.7 %cholesky.393 = f32[128,128]{1,0:T(8,128)S(1)} custom-call(f32[128,128]{1,0:T(8,128)S(1)} %fusion.104), custom_call_target="Cholesky" | custom-call | tf_op jit(solution)/shard_map/jit(cholesky)/cholesky | solution.py:39
  502.8 9.9 %custom-call.41 = f32[1,128,128]{1,2,0:T(8,128)S(1)} custom-call(f32[1,128,128]{2,1,0:T(8,128)S(1)} %fusion.69), custom_call_target="InvertDiagBlocksLowerTriangular" | custom-call | tf_op jit(solution)/shard_map/jit(_solve_triangular)/triangular_solve/custom-call.3 | solution.py:40
  515.4 21.0 %collective-permute-done.2 = f32[128,1536]{1,0:T(8,128)S(1)} collective-permute-done((f32[128,1536]{1,0:T(8,128)}, f32[128,1536]{1,0:T(8,128)S(1)}, u32[]{:S(2)}, u32[]{:S(2)}) %collective-permute-start.2) | collective-permute-done | bytes 786464 | tf_op jit(solution)/shard_map/ppermute | solution.py:20
  540.0 42.5 %all-reduce.14.cloned.1.call-done = (f32[128,128]{1,0:T(8,128)}, f32[128,128]{0,1:T(8,128)}, f32[128,128]{0,1:T(8,128)}) async-done(((f32[128,128]{1,0:T(8,128)}, f32[128,128]{0,1:T(8,128)}, f32[128,128]{0,1:T(8,128)}), (f32[128,128]{1,0:T(8,128)}, f32[128,128]{0,1:T(8,128)}, f32[128,128]{0,1:T(8,128)})) %all-reduce.14.cloned.1.call-update) | async-done | bytes 196624 | tf_op jit(solution)/shard_map/psum | solution.py:46
  586.1 11.7 %cholesky.470 = f32[128,128]{1,0:T(8,128)S(1)} custom-call(f32[128,128]{1,0:T(8,128)S(1)} %fusion.87), custom_call_target="Cholesky" | custom-call | tf_op jit(solution)/shard_map/jit(cholesky)/cholesky | solution.py:32
  599.0 9.8 %custom-call.42 = f32[1,128,128]{1,2,0:T(8,128)S(1)} custom-call(f32[1,128,128]{2,1,0:T(8,128)S(1)} %fusion.70), custom_call_target="InvertDiagBlocksLowerTriangular" | custom-call | tf_op jit(solution)/shard_map/jit(_solve_triangular)/triangular_solve/custom-call.3 | solution.py:33
  610.7 11.7 %cholesky.481 = f32[128,128]{1,0:T(8,128)S(1)} custom-call(f32[128,128]{1,0:T(8,128)S(1)} %fusion.84), custom_call_target="Cholesky" | custom-call | tf_op jit(solution)/shard_map/jit(cholesky)/cholesky | solution.py:37
  626.7 11.7 %cholesky.492 = f32[128,128]{1,0:T(8,128)S(1)} custom-call(f32[128,128]{1,0:T(8,128)S(1)} %fusion.83), custom_call_target="Cholesky" | custom-call | tf_op jit(solution)/shard_map/jit(cholesky)/cholesky | solution.py:39
  653.8 42.6 %all-reduce.12.cloned.1.call-done = (f32[128,256]{1,0:T(8,128)}, f32[128,128]{0,1:T(8,128)}) async-done(((f32[128,256]{1,0:T(8,128)}, f32[128,128]{0,1:T(8,128)}), (f32[128,256]{1,0:T(8,128)}, f32[128,128]{0,1:T(8,128)})) %all-reduce.12.cloned.1.call-update) | async-done | bytes 196624 | tf_op jit(solution)/shard_map/psum | solution.py:96
  708.5 11.7 %cholesky.503 = f32[128,128]{1,0:T(8,128)S(1)} custom-call(f32[128,128]{1,0:T(8,128)S(1)} %copy.70), custom_call_target="Cholesky" | custom-call | tf_op jit(solution)/shard_map/jit(cholesky)/cholesky | solution.py:108
  (292 shorter events, 179.8 us)
Async XLA Ops:
  6.5 49.5 %all-reduce.10.cloned.1.call-start = ((), (), s32[]{:S(2)}) async-start(), calls=%async_computation | async-start | bytes 524288 | tf_op jit(solution)/shard_map/psum | solution.py:76
  9.1 164.0 %all-reduce.18.cloned.1.call-start = ((), (), s32[]{:S(2)}) async-start(), calls=%async_computation.4 | async-start | bytes 524288 | tf_op jit(solution)/shard_map/psum | solution.py:46
  56.1 25.1 %copy-start.6 = (f32[1,256,256]{2,1,0:T(8,128)S(1)}, f32[1,256,256]{2,1,0:T(8,128)}, u32[]{:S(2)}) copy-start(f32[1,256,256]{2,1,0:T(8,128)} %all-reduce.10.cloned.1.call-done) | copy-start | bytes 786436
  95.1 27.4 %copy-start.2 = (bf16[256,1536]{1,0:T(8,128)(2,1)S(1)}, bf16[256,1536]{1,0:T(8,128)(2,1)}, u32[]{:S(2)}) copy-start(bf16[256,1536]{1,0:T(8,128)(2,1)} %param.8) | copy-start | bytes 2359300
  123.0 2.4 collective-permute-start
  129.6 245.3 %all-reduce.16.cloned.1.call-start = ((), (), s32[]{:S(2)}) async-start(), calls=%async_computation.3 | async-start | bytes 655360 | tf_op jit(solution)/shard_map/psum | solution.py:46
  173.1 2.9 copy-start.8
  173.1 2.9 copy-start.9
  173.1 2.9 copy-start.12
  173.1 3.3 copy-start.11
  307.1 21.6 %copy-start = (f32[128,1536]{1,0:T(8,128)}, f32[128,1536]{1,0:T(8,128)S(1)}, u32[]{:S(2)}) copy-start(f32[128,1536]{1,0:T(8,128)S(1)} %fusion.3) | copy-start | bytes 2359300
  307.1 18.8 %collective-permute-start.1 = (f32[128,1536]{1,0:T(8,128)S(1)}, f32[128,1536]{1,0:T(8,128)S(1)}, u32[]{:S(2)}, u32[]{:S(2)}) collective-permute-start(f32[128,1536]{1,0:T(8,128)S(1)} %fusion.3), channel_id=1, source_target_pairs={{0,8},{8,0},{4,12},{12,4},{16,24},{24,16},{20,28},{28,20},{1,9},{9... | collective-permute-start | bytes 2359304 | tf_op jit(solution)/shard_map/ppermute | solution.py:20
  330.2 252.4 %all-reduce.14.cloned.1.call-start = ((), (), s32[]{:S(2)}) async-start(), calls=%async_computation.2 | async-start | bytes 393216 | tf_op jit(solution)/shard_map/psum | solution.py:46
  374.9 2.3 copy-start.14
  374.9 2.3 copy-start.18
  402.3 29.0 %copy-start.7 = (f32[128,128]{0,1:T(8,128)S(1)}, f32[128,128]{0,1:T(8,128)}, u32[]{:S(2)}) copy-start(f32[128,128]{0,1:T(8,128)} %get-tuple-element.19) | copy-start | bytes 196612
  402.4 29.0 %copy-start.10 = (f32[128,128]{0,1:T(8,128)S(1)}, f32[128,128]{0,1:T(8,128)}, u32[]{:S(2)}) copy-start(f32[128,128]{0,1:T(8,128)} %get-tuple-element.18) | copy-start | bytes 196612
  402.4 29.0 %copy-start.16 = (f32[128,128]{0,1:T(8,128)S(1)}, f32[128,128]{0,1:T(8,128)}, u32[]{:S(2)}) copy-start(f32[128,128]{0,1:T(8,128)} %get-tuple-element.20) | copy-start | bytes 196612
  470.4 27.4 %copy-start.1 = (f32[128,1536]{1,0:T(8,128)S(1)}, f32[128,1536]{1,0:T(8,128)}, u32[]{:S(2)}) copy-start(f32[128,1536]{1,0:T(8,128)} %copy-done) | copy-start | bytes 2359300
  499.7 36.7 %collective-permute-start.2 = (f32[128,1536]{1,0:T(8,128)}, f32[128,1536]{1,0:T(8,128)S(1)}, u32[]{:S(2)}, u32[]{:S(2)}) collective-permute-start(f32[128,1536]{1,0:T(8,128)} %fusion.7), channel_id=1, source_target_pairs={{0,16},{16,0},{4,20},{20,4},{8,24},{24,8},{12,28},{28,12},{1,17},{... | collective-permute-start | bytes 2359304 | tf_op jit(solution)/shard_map/ppermute | solution.py:20
  536.4 1.4 copy-start.4
  539.3 157.2 %all-reduce.12.cloned.1.call-start = ((), (), s32[]{:S(2)}) async-start(), calls=%async_computation.1 | async-start | bytes 393216 | tf_op jit(solution)/shard_map/psum | solution.py:96
  582.5 2.3 copy-start.13
  582.5 2.3 copy-start.17
  610.6 39.4 %copy-start.5 = (f32[128,1536]{1,0:T(8,128)S(1)}, f32[128,1536]{1,0:T(8,128)}, u32[]{:S(2)}) copy-start(f32[128,1536]{1,0:T(8,128)} %copy-done.4) | copy-start | bytes 2359300
  650.0 1.1 copy-start.3
  705.9 1.9 copy-start.15
  707.2 24.2 %copy-start.19 = (f32[128,256]{1,0:T(8,128)S(1)}, f32[128,256]{1,0:T(8,128)}, u32[]{:S(2)}) copy-start(f32[128,256]{1,0:T(8,128)} %get-tuple-element.10) | copy-start | bytes 393220
Sparse Core Ops, SparseCore 0:
  10.3 45.7 all-reduce.9
  129.7 43.3 all-reduce.17
  330.3 44.6 all-reduce.15
  539.4 43.1 all-reduce.13
  653.8 42.6 all-reduce.11
where the time goes:
time: 750 us; the launch traced here: 740 us
  other arithmetic  385 us (51%)
  waiting for transfers between devices  255 us (34%)
  matrix products  66.9 us (9%)
  between operations  23.9 us (3%)
    psum x3, waiting for transfers between devices, combine(): lax.psum((product(earlier, earlier.T), product(earlier, later.T), product...  130 us
    another operation x18, other arithmetic, reduce_gram(): root_factor = jnp.linalg.cholesky(quotient)  74.9 us
    another operation x18, other arithmetic, reduce_gram(): lower_factor = jnp.linalg.cholesky(inner_gram)  74.6 us
    another operation x18, other arithmetic, reduce_gram(): factor = jnp.linalg.cholesky(product(image_cols.T, image_cols))  74.4 us
    another operation x12, other arithmetic, reduce_gram(): jax.scipy.linalg.solve_triangular(lower_factor, product(root_factor.T, su...  63.4 us
    another operation x12, other arithmetic, reduce_gram(): jax.scipy.linalg.solve_triangular(factor, image_cols.T, lower=True)  62.9 us
    dot_general x89, matrix products, product(): return jnp.dot(left_matrix, right_matrix, precision=precise)  57.2 us
    psum x1, waiting for transfers between devices, on_device(): slab_grams = lax.psum(partial_grams, 'feat')  46.9 us
  transfers between devices with their start and end apart: 8, of which 8 were waited for; matrix products, arithmetic and copies ran while one was open for 3% of the time, Pallas kernels for 0%

commit v1 on v0

v1 whole, which is shorter than its diff:
```python
import functools

import jax
import jax.numpy as jnp
from jax import lax
from jax.experimental import pallas as pl
from jax.experimental.pallas import tpu as pltpu
from jax.sharding import PartitionSpec as P

RANK = 128
ROOT_STEPS = 12
PANEL = 16
MESH = pl.DeviceIdType.MESH
HIGHEST = lax.Precision.HIGHEST


def mm(a, b):
    return jnp.dot(a, b, precision=HIGHEST, preferred_element_type=jnp.float32)


def mm_t(a, b):
    return lax.dot_general(
        a, b, (((1,), (1,)), ((), ())), precision=HIGHEST, preferred_element_type=jnp.float32
    )


def split_3(x):
    high = x.astype(jnp.bfloat16)
    rest = x - high.astype(jnp.float32)
    middle = rest.astype(jnp.bfloat16)
    low = (rest - middle.astype(jnp.float32)).astype(jnp.bfloat16)
    return high, middle, low


def eye():
    rows = lax.broadcasted_iota(jnp.int32, (RANK, RANK), 0)
    columns = lax.broadcasted_iota(jnp.int32, (RANK, RANK), 1)
    return jnp.where(rows == columns, 1.0, 0.0).astype(jnp.float32)


def trace(matrix):
    size = matrix.shape[0]
    rows = lax.broadcasted_iota(jnp.int32, (size, size), 0)
    columns = lax.broadcasted_iota(jnp.int32, (size, size), 1)
    kept = jnp.where(rows == columns, matrix, 0.0)
    return jnp.sum(jnp.sum(kept, axis=1, keepdims=True), axis=0, keepdims=True)


def factorize(matrices, work):
    count = len(matrices)
    for k in range(count):
        work[k, :, :RANK] = matrices[k]
        work[k, :, RANK:] = eye()
    lane = lax.broadcasted_iota(jnp.int32, (PANEL, RANK), 1)
    sub = lax.broadcasted_iota(jnp.int32, (PANEL, RANK), 0)

    def step(index, carry):
        first = pl.multiple_of(index * PANEL, PANEL)
        left = [work[k, pl.ds(first, PANEL), :RANK] for k in range(count)]
        right = [work[k, pl.ds(first, PANEL), RANK:] for k in range(count)]
        columns = [
            [
                jnp.broadcast_to(
                    jnp.sum(jnp.where(lane == first + c, left[k], 0.0), axis=1, keepdims=True),
                    (PANEL, RANK),
                )
                for c in range(PANEL)
            ]
            for k in range(count)
        ]
        for i in range(PANEL):
            for k in range(count):
                scale = lax.rsqrt(columns[k][i][i : i + 1, :])
                factor = jnp.where(sub > i, columns[k][i], 0.0) * scale
                for c in range(i + 1, PANEL):
                    columns[k][c] -= factor * (columns[k][c][i : i + 1, :] * scale)
                row_left = left[k][i : i + 1, :] * scale
                row_right = right[k][i : i + 1, :] * scale
                left[k] = jnp.where(sub == i, row_left, left[k] - factor * row_left)
                right[k] = jnp.where(sub == i, row_right, right[k] - factor * row_right)
        for k in range(count):
            work[k, pl.ds(first, PANEL), :RANK] = left[k]
            work[k, pl.ds(first, PANEL), RANK:] = right[k]
            h, m, l = split_3(jnp.where(lane >= first + PANEL, left[k], 0.0))
            lh, lm, ll = split_3(left[k])
            rh, rm, rl = split_3(right[k])
            h, m, l = (part.astype(jnp.float32) for part in (h, m, l))
            lhs = jnp.concatenate([h, h, m, m, h, l, jnp.zeros((2 * PANEL, RANK), jnp.float32)], axis=0)
            lhs = lhs.T.astype(jnp.bfloat16)
            for part, (a, b, c) in enumerate([(lh, lm, ll), (rh, rm, rl)]):
                rhs = jnp.concatenate([a, b, a, b, c, a, jnp.zeros((2 * PANEL, RANK), jnp.bfloat16)], axis=0)
                work[k, :, part * RANK : (part + 1) * RANK] -= jnp.dot(
                    lhs, rhs, preferred_element_type=jnp.float32
                )
        return carry

    lax.fori_loop(0, RANK // PANEL, step, 0)
    rows = lax.broadcasted_iota(jnp.int32, (RANK, RANK), 0)
    cols = lax.broadcasted_iota(jnp.int32, (RANK, RANK), 1)
    return [
        (jnp.where(cols >= rows, work[k, :, :RANK], 0.0), work[k, :, RANK:]) for k in range(count)
    ]


def reduce_grams(grams, work):
    images = [(gram[:RANK, :] + gram[RANK:, :]) * 0.7071067811865476 for gram in grams]
    factors = factorize([mm_t(image, image) for image in images], work)
    bases = [mm(inverse, image) for (_, inverse), image in zip(factors, images)]
    quotients = [mm_t(mm(basis, gram), basis) for basis, gram in zip(bases, grams)]
    quotients = [0.5 * (quotient + quotient.T) for quotient in quotients]
    tails = [(trace(gram) - trace(quotient)) / RANK for gram, quotient in zip(grams, quotients)]
    uppers = [upper for upper, _ in factorize(quotients, work)]
    factors = factorize([mm_t(u, u) + tail * eye() for u, tail in zip(uppers, tails)], work)
    out = []
    for (_, inverse), upper, basis, gram in zip(factors, uppers, bases, grams):
        mixing = mm(mm(inverse, upper), basis)
        out.append((mixing, mm_t(mm(mixing, gram), mixing)))
    return out


def kernel(levels, feats, ridge_ref, rows_ref, out_ref, *scratch):
    work, tree, prefix, partner, grams, partner_grams = scratch[:6]
    slab_slots = scratch[6]
    level_slots = scratch[7 : 7 + levels]
    last_slots = scratch[7 + levels]
    send_sem, recv_sem, pair_send, pair_recv = scratch[8 + levels :]
    seq = lax.axis_index("seq")
    feat = lax.axis_index("feat")
    width = rows_ref.shape[1]

    def bit_of(level):
        return lax.rem(seq // (1 << level), 2)

    def sibling(level):
        return seq + (1 << level) - 2 * (1 << level) * bit_of(level)

    barrier = pltpu.get_barrier_semaphore()
    for offset in range(1, feats):
        pl.semaphore_signal(
            barrier, inc=1, device_id=(seq, lax.rem(feat + offset, feats)), device_id_type=MESH
        )
    for level in range(levels):
        pl.semaphore_signal(
            barrier, inc=1, device_id=(sibling(level), feat), device_id_type=MESH
        )
    pl.semaphore_wait(barrier, feats - 1 + levels)

    def send_sum(slots, phase):
        copies = []
        for offset in range(1, feats):
            copy = pltpu.make_async_remote_copy(
                src_ref=slots.at[feat],
                dst_ref=slots.at[feat],
                send_sem=send_sem.at[phase, offset],
                recv_sem=recv_sem.at[phase, offset],
                device_id=(seq, lax.rem(feat + offset, feats)),
                device_id_type=MESH,
            )
            copy.start()
            copies.append(copy)
        return copies

    def finish_sum(slots, copies):
        for copy in copies:
            copy.wait()
        total = slots[0]
        for index in range(1, feats):
            total = total + slots[index]
        return total

    rows = rows_ref[...]
    slab_slots[feat] = lax.dot_general(
        rows, rows, (((1,), (1,)), ((), ())), preferred_element_type=jnp.float32
    )
    gram = finish_sum(slab_slots, send_sum(slab_slots, 0))
    ((mixing, own_gram),) = reduce_grams([gram], work)
    h, m, l = split_3(mixing)
    sketch = (
        jnp.dot(l, rows, preferred_element_type=jnp.float32)
        + jnp.dot(m, rows, preferred_element_type=jnp.float32)
        + jnp.dot(h, rows, preferred_element_type=jnp.float32)
    )
    tree[0] = sketch
    prefix[...] = sketch
    grams[0] = own_gram
    prefix_gram = own_gram

    for level in range(levels):
        copies = []
        for index, (source, target) in enumerate(
            [(tree.at[level], partner.at[level]), (grams.at[level], partner_grams.at[level])]
        ):
            copy = pltpu.make_async_remote_copy(
                src_ref=source,
                dst_ref=target,
                send_sem=pair_send.at[level, index],
                recv_sem=pair_recv.at[level, index],
                device_id=(sibling(level), feat),
                device_id_type=MESH,
            )
            copy.start()
            copies.append(copy)
        for copy in copies:
            copy.wait()
        slots = level_slots[level]
        with_prefix = level > 0
        with_tree = level + 1 < levels or level == 0
        lefts = []
        if with_tree:
            lefts.append((tree.at[level], grams[level]))
        if with_prefix:
            lefts.append((prefix, prefix_gram))
        for index, (left, _) in enumerate(lefts):
            slots[feat, index * RANK : (index + 1) * RANK, :] = mm_t(
                left[...], partner[level]
            )
        crosses = finish_sum(slots, send_sum(slots, 1 + level))
        other = partner_grams[level]
        stacked = []
        for index, (_, left_gram) in enumerate(lefts):
            cross = crosses[index * RANK : (index + 1) * RANK]
            stacked.append(
                jnp.concatenate(
                    [
                        jnp.concatenate([left_gram, cross], 1),
                        jnp.concatenate([cross.T, other], 1),
                    ],
                    0,
                )
            )
        results = reduce_grams(stacked, work)
        merged = []
        for (left, _), (mixing, new_gram) in zip(lefts, results):
            merged.append(
                (mm(mixing[:, :RANK], left[...]) + mm(mixing[:, RANK:], partner[level]), new_gram)
            )
        keep = bit_of(level) == 1
        prefix[...] = jnp.where(keep, merged[-1][0], prefix[...])
        prefix_gram = jnp.where(keep, merged[-1][1], prefix_gram)
        if level + 1 < levels:
            tree[level + 1] = merged[0][0]
            grams[level + 1] = merged[0][1]

    ridge = ridge_ref[0, 0]
    seen_rows = ((seq + 1) * rows_ref.shape[0]).astype(jnp.float32)
    seen = jnp.full((1, 1), seen_rows * ridge, jnp.float32)
    half_basis = (prefix[...] * lax.rsqrt(seen)).astype(jnp.bfloat16)
    last_slots[feat] = lax.dot_general(
        rows, half_basis, (((1,), (1,)), ((), ())), preferred_element_type=jnp.float32
    )
    copies = send_sum(last_slots, 1 + levels)
    shifted = eye() + prefix_gram / seen
    norm = jnp.sqrt(
        jnp.sum(jnp.sum(shifted * shifted, axis=1, keepdims=True), axis=0, keepdims=True)
    )

    work[0, :, :RANK] = shifted / norm
    work[0, :, RANK:] = eye()

    def root_step(index, carry):
        current, other = work[0, :, :RANK], work[0, :, RANK:]
        middle = 1.5 * eye() - 0.5 * mm(other, current)
        work[0, :, :RANK] = mm(current, middle)
        work[0, :, RANK:] = mm(middle, other)
        return carry

    lax.fori_loop(0, ROOT_STEPS, root_step, 0)
    current = work[0, :, :RANK]
    total_gram = shifted + current * jnp.sqrt(norm)
    total_gram = 0.5 * (total_gram + total_gram.T)
    ((_, inverse),) = factorize([total_gram], work)
    projection = finish_sum(last_slots, copies)
    coefficients = mm(mm_t(projection, inverse), inverse).astype(jnp.bfloat16)
    restored = jnp.dot(coefficients, half_basis, preferred_element_type=jnp.float32)
    out_ref[...] = (
        (rows.astype(jnp.float32) - restored) * lax.rsqrt(jnp.full((1, 1), ridge, jnp.float32))
    ).astype(jnp.bfloat16)


def on_device(activations, ridge_scale):
    tokens, width = activations.shape
    feats = lax.axis_size("feat")
    levels = lax.axis_size("seq").bit_length() - 1
    wide = (RANK, width)
    square = (RANK, RANK)
    f32 = jnp.float32
    scratch = [
        pltpu.VMEM((2, RANK, 2 * RANK), f32),
        pltpu.VMEM((levels,) + wide, f32),
        pltpu.VMEM(wide, f32),
        pltpu.VMEM((levels,) + wide, f32),
        pltpu.VMEM((levels,) + square, f32),
        pltpu.VMEM((levels,) + square, f32),
        pltpu.VMEM((feats, tokens, tokens), f32),
    ]
    for level in range(levels):
        count = 2 if 0 < level < levels - 1 else 1
        scratch.append(pltpu.VMEM((feats, count * RANK, RANK), f32))
    scratch.append(pltpu.VMEM((feats, tokens, RANK), f32))
    scratch += [
        pltpu.SemaphoreType.DMA((levels + 2, feats)),
        pltpu.SemaphoreType.DMA((levels + 2, feats)),
        pltpu.SemaphoreType.DMA((levels, 2)),
        pltpu.SemaphoreType.DMA((levels, 2)),
    ]
    return pl.pallas_call(
        functools.partial(kernel, levels, feats),
        out_shape=jax.ShapeDtypeStruct(activations.shape, activations.dtype),
        in_specs=[
            pl.BlockSpec(memory_space=pltpu.SMEM),
            pl.BlockSpec(memory_space=pltpu.VMEM),
        ],
        out_specs=pl.BlockSpec(memory_space=pltpu.VMEM),
        scratch_shapes=scratch,
        compiler_params=pltpu.CompilerParams(
            collective_id=0, has_side_effects=True, vmem_limit_bytes=60 * 1024 * 1024
        ),
    )(ridge_scale.reshape(1, 1), activations)


def solution(mesh):
    placed = (P("seq", "feat"), P())
    return jax.shard_map(
        on_device, mesh=mesh, in_specs=placed, out_specs=P("seq", "feat"), check_vma=False
    )
```

time: 750 us -> 183 us (0.24); the launches traced: 740 us -> 183 us
  other arithmetic: 385 us -> 0 us
  waiting for transfers between devices: 255 us -> 0 us
  Pallas kernels: 0 us -> 180 us
  matrix products: 66.9 us -> 0 us
  between operations: 23.9 us -> 0.66 us
    another operation x83 -> x0, other arithmetic: 373 us -> none  [the longest x18 74.9 us: reduce_gram(): root_factor = jnp.linalg.cholesky(quotient)]
    psum x5 -> x0, waiting for transfers between devices: 220 us -> none  [the longest x3 130 us: combine(): lax.psum((product(earlier, earlier.T), product(earlier, later.T), product...]
    pallas_call x0 -> x1, Pallas kernels: none -> 180 us  [on_device(): pl.pallas_call(functools.partial(kernel, levels, feats), out_shape=jax.Sh...]
    dot_general x93 -> x0, matrix products: 62.5 us -> none  [the longest x89 57.2 us: product(): return jnp.dot(left_matrix, right_matrix, precision=precise)]
    ppermute x3 -> x0, waiting for transfers between devices: 35 us -> none  [partner_2(): return lax.ppermute(block, axis, route)]
    reduce_sum x12 -> x0, other arithmetic: 8.66 us -> none  [the longest x11 7.2 us: reduce_gram(): tail_mass = (jnp.trace(stacked_gram) - jnp.trace(quotient)) / rank_size]
  transfers between devices with their start and end apart: 8 -> 0, of which waited for: 8 -> 0; matrix products, arithmetic and copies ran while one was open for 3% -> 0% of each run, Pallas kernels for 0% -> 0%
where the time goes in v1:
time: 183 us
  Pallas kernels  180 us (98%)
  local copies, waits for them, and re-layouts  2.06 us (1%)
    pallas_call x1, Pallas kernels, on_device(): pl.pallas_call(functools.partial(kernel, levels, feats), out_shape=jax.Sh...  180 us

profile of v1, /device:TPU:0, one launch (start us, length us, event | category | flops | bytes accessed | tf_op | source)
XLA Modules:
  0.0 182.8 jit_solution(10527316830355757645)
XLA Ops:
  0.7 180.1 %shard_map.28 = bf16[256,1536]{1,0:T(8,128)(2,1)} custom-call(f32[1,1]{1,0:T(1,128)} %bitcast.1.ridge_ref, bf16[256,1536]{1,0:T(8,128)(2,1)} %rows_ref.1), custom_call_target="tpu_custom_call" | custom-call | tf_op jit(solution)/shard_map/pallas_call | solution.py:306
  180.8 2.1 %copy.5 = bf16[256,1536]{1,0:T(8,128)(2,1)} copy(bf16[256,1536]{1,0:T(8,128)(2,1)} %shard_map.28) | data formatting | bytes 1572864

commit v2 on v1

--- a/solution.py
+++ b/solution.py
@@ -46,18 +46,19 @@
     return jnp.sum(jnp.sum(kept, axis=1, keepdims=True), axis=0, keepdims=True)
 
 
-def factorize(matrices, work):
+def factorize(matrices, work, inverse=True):
     count = len(matrices)
     for k in range(count):
         work[k, :, :RANK] = matrices[k]
-        work[k, :, RANK:] = eye()
+        if inverse:
+            work[k, :, RANK:] = eye()
     lane = lax.broadcasted_iota(jnp.int32, (PANEL, RANK), 1)
     sub = lax.broadcasted_iota(jnp.int32, (PANEL, RANK), 0)
 
     def step(index, carry):
         first = pl.multiple_of(index * PANEL, PANEL)
         left = [work[k, pl.ds(first, PANEL), :RANK] for k in range(count)]
-        right = [work[k, pl.ds(first, PANEL), RANK:] for k in range(count)]
+        right = [work[k, pl.ds(first, PANEL), RANK:] for k in range(count) if inverse]
         columns = [
             [
                 jnp.broadcast_to(
@@ -75,19 +76,20 @@
                 for c in range(i + 1, PANEL):
                     columns[k][c] -= factor * (columns[k][c][i : i + 1, :] * scale)
                 row_left = left[k][i : i + 1, :] * scale
-                row_right = right[k][i : i + 1, :] * scale
                 left[k] = jnp.where(sub == i, row_left, left[k] - factor * row_left)
-                right[k] = jnp.where(sub == i, row_right, right[k] - factor * row_right)
+                if inverse:
+                    row_right = right[k][i : i + 1, :] * scale
+                    right[k] = jnp.where(sub == i, row_right, right[k] - factor * row_right)
         for k in range(count):
             work[k, pl.ds(first, PANEL), :RANK] = left[k]
-            work[k, pl.ds(first, PANEL), RANK:] = right[k]
+            if inverse:
+                work[k, pl.ds(first, PANEL), RANK:] = right[k]
             h, m, l = split_3(jnp.where(lane >= first + PANEL, left[k], 0.0))
-            lh, lm, ll = split_3(left[k])
-            rh, rm, rl = split_3(right[k])
+            sides = [split_3(side) for side in ([left[k], right[k]] if inverse else [left[k]])]
             h, m, l = (part.astype(jnp.float32) for part in (h, m, l))
             lhs = jnp.concatenate([h, h, m, m, h, l, jnp.zeros((2 * PANEL, RANK), jnp.float32)], axis=0)
             lhs = lhs.T.astype(jnp.bfloat16)
-            for part, (a, b, c) in enumerate([(lh, lm, ll), (rh, rm, rl)]):
+            for part, (a, b, c) in enumerate(sides):
                 rhs = jnp.concatenate([a, b, a, b, c, a, jnp.zeros((2 * PANEL, RANK), jnp.bfloat16)], axis=0)
                 work[k, :, part * RANK : (part + 1) * RANK] -= jnp.dot(
                     lhs, rhs, preferred_element_type=jnp.float32
@@ -98,7 +100,8 @@
     rows = lax.broadcasted_iota(jnp.int32, (RANK, RANK), 0)
     cols = lax.broadcasted_iota(jnp.int32, (RANK, RANK), 1)
     return [
-        (jnp.where(cols >= rows, work[k, :, :RANK], 0.0), work[k, :, RANK:]) for k in range(count)
+        (jnp.where(cols >= rows, work[k, :, :RANK], 0.0), work[k, :, RANK:] if inverse else None)
+        for k in range(count)
     ]
 
 
@@ -109,7 +112,7 @@
     quotients = [mm_t(mm(basis, gram), basis) for basis, gram in zip(bases, grams)]
     quotients = [0.5 * (quotient + quotient.T) for quotient in quotients]
     tails = [(trace(gram) - trace(quotient)) / RANK for gram, quotient in zip(grams, quotients)]
-    uppers = [upper for upper, _ in factorize(quotients, work)]
+    uppers = [upper for upper, _ in factorize(quotients, work, False)]
     factors = factorize([mm_t(u, u) + tail * eye() for u, tail in zip(uppers, tails)], work)
     out = []
     for (_, inverse), upper, basis, gram in zip(factors, uppers, bases, grams):
@@ -119,11 +122,11 @@
 
 
 def kernel(levels, feats, ridge_ref, rows_ref, out_ref, *scratch):
-    work, tree, prefix, partner, grams, partner_grams = scratch[:6]
-    slab_slots = scratch[6]
-    level_slots = scratch[7 : 7 + levels]
-    last_slots = scratch[7 + levels]
-    send_sem, recv_sem, pair_send, pair_recv = scratch[8 + levels :]
+    work, tree, prefix, partner = scratch[:4]
+    slab_slots = scratch[4]
+    level_slots = scratch[5 : 5 + levels]
+    last_slots = scratch[5 + levels]
+    send_sem, recv_sem, pair_send, pair_recv = scratch[6 + levels :]
     seq = lax.axis_index("seq")
     feat = lax.axis_index("feat")
     width = rows_ref.shape[1]
@@ -168,6 +171,26 @@
             total = total + slots[index]
         return total
 
+    def fetch(level):
+        for index, hop in enumerate(range(level, -1, -1)):
+            source = tree if hop == level else partner
+            bits = hop if hop == level else hop + 1
+            size = RANK >> bits
+            first = 0
+            for bit in range(bits):
+                first = first + bit_of(bit) * (RANK >> (bit + 1))
+            span = pl.ds(pl.multiple_of(first, size), size) if bits else pl.ds(0, RANK)
+            copy = pltpu.make_async_remote_copy(
+                src_ref=source.at[level, span],
+                dst_ref=partner.at[level, span],
+                send_sem=pair_send.at[level, index],
+                recv_sem=pair_recv.at[level, index],
+                device_id=(sibling(hop), feat),
+                device_id_type=MESH,
+            )
+            copy.start()
+            copy.wait()
+
     rows = rows_ref[...]
     slab_slots[feat] = lax.dot_general(
         rows, rows, (((1,), (1,)), ((), ())), preferred_element_type=jnp.float32
@@ -180,42 +203,27 @@
         + jnp.dot(m, rows, preferred_element_type=jnp.float32)
         + jnp.dot(h, rows, preferred_element_type=jnp.float32)
     )
-    tree[0] = sketch
+    tree[0, :, :width] = sketch
+    tree[0, :, width:] = own_gram
     prefix[...] = sketch
-    grams[0] = own_gram
     prefix_gram = own_gram
 
     for level in range(levels):
-        copies = []
-        for index, (source, target) in enumerate(
-            [(tree.at[level], partner.at[level]), (grams.at[level], partner_grams.at[level])]
-        ):
-            copy = pltpu.make_async_remote_copy(
-                src_ref=source,
-                dst_ref=target,
-                send_sem=pair_send.at[level, index],
-                recv_sem=pair_recv.at[level, index],
-                device_id=(sibling(level), feat),
-                device_id_type=MESH,
-            )
-            copy.start()
-            copies.append(copy)
-        for copy in copies:
-            copy.wait()
+        fetch(level)
         slots = level_slots[level]
         with_prefix = level > 0
         with_tree = level + 1 < levels or level == 0
         lefts = []
         if with_tree:
-            lefts.append((tree.at[level], grams[level]))
+            lefts.append((tree.at[level, :, :width], tree[level, :, width:]))
         if with_prefix:
             lefts.append((prefix, prefix_gram))
         for index, (left, _) in enumerate(lefts):
             slots[feat, index * RANK : (index + 1) * RANK, :] = mm_t(
-                left[...], partner[level]
+                left[...], partner[level, :, :width]
             )
         crosses = finish_sum(slots, send_sum(slots, 1 + level))
-        other = partner_grams[level]
+        other = partner[level, :, width:]
         stacked = []
         for index, (_, left_gram) in enumerate(lefts):
             cross = crosses[index * RANK : (index + 1) * RANK]
@@ -232,14 +240,14 @@
         merged = []
         for (left, _), (mixing, new_gram) in zip(lefts, results):
             merged.append(
-                (mm(mixing[:, :RANK], left[...]) + mm(mixing[:, RANK:], partner[level]), new_gram)
+                (mm(mixing[:, :RANK], left[...]) + mm(mixing[:, RANK:], partner[level, :, :width]), new_gram)
             )
         keep = bit_of(level) == 1
         prefix[...] = jnp.where(keep, merged[-1][0], prefix[...])
         prefix_gram = jnp.where(keep, merged[-1][1], prefix_gram)
         if level + 1 < levels:
-            tree[level + 1] = merged[0][0]
-            grams[level + 1] = merged[0][1]
+            tree[level + 1, :, :width] = merged[0][0]
+            tree[level + 1, :, width:] = merged[0][1]
 
     ridge = ridge_ref[0, 0]
     seen_rows = ((seq + 1) * rows_ref.shape[0]).astype(jnp.float32)
@@ -282,15 +290,12 @@
     feats = lax.axis_size("feat")
     levels = lax.axis_size("seq").bit_length() - 1
     wide = (RANK, width)
-    square = (RANK, RANK)
     f32 = jnp.float32
     scratch = [
         pltpu.VMEM((2, RANK, 2 * RANK), f32),
-        pltpu.VMEM((levels,) + wide, f32),
+        pltpu.VMEM((levels, RANK, width + RANK), f32),
         pltpu.VMEM(wide, f32),
-        pltpu.VMEM((levels,) + wide, f32),
-        pltpu.VMEM((levels,) + square, f32),
-        pltpu.VMEM((levels,) + square, f32),
+        pltpu.VMEM((levels, RANK, width + RANK), f32),
         pltpu.VMEM((feats, tokens, tokens), f32),
     ]
     for level in range(levels):
@@ -300,8 +305,8 @@
     scratch += [
         pltpu.SemaphoreType.DMA((levels + 2, feats)),
         pltpu.SemaphoreType.DMA((levels + 2, feats)),
-        pltpu.SemaphoreType.DMA((levels, 2)),
-        pltpu.SemaphoreType.DMA((levels, 2)),
+        pltpu.SemaphoreType.DMA((levels, levels)),
+        pltpu.SemaphoreType.DMA((levels, levels)),
     ]
     return pl.pallas_call(
         functools.partial(kernel, levels, feats),

time: 183 us -> 157 us (0.86)
  Pallas kernels: 180 us -> 154 us
    pallas_call x1, Pallas kernels: 180 us -> 154 us  [on_device(): pl.pallas_call(functools.partial(kernel, levels, feats), out_shape=jax.Sh...]
where the time goes in v2:
time: 157 us; the launch traced here: 156 us
  Pallas kernels  154 us (98%)
  local copies, waits for them, and re-layouts  2.06 us (1%)
    pallas_call x1, Pallas kernels, on_device(): pl.pallas_call(functools.partial(kernel, levels, feats), out_shape=jax.Sh...  154 us

profile of v2, /device:TPU:0, one launch (start us, length us, event | category | flops | bytes accessed | tf_op | source)
XLA Modules:
  0.0 156.4 jit_solution(8615627440963282146)
XLA Ops:
  0.7 153.7 %shard_map.28 = bf16[256,1536]{1,0:T(8,128)(2,1)} custom-call(f32[1,1]{1,0:T(1,128)} %bitcast.1.ridge_ref, bf16[256,1536]{1,0:T(8,128)(2,1)} %rows_ref.1), custom_call_target="tpu_custom_call" | custom-call | tf_op jit(solution)/shard_map/pallas_call | solution.py:311
  154.4 2.1 %copy.5 = bf16[256,1536]{1,0:T(8,128)(2,1)} copy(bf16[256,1536]{1,0:T(8,128)(2,1)} %shard_map.28) | data formatting | bytes 1572864
